TPU v7x, 32 devices: a whole 2x2x4 slice. The times are simulated.
32 devices in a mesh: ends: 2 (over x), dp: 4 (over y, core), tp: 4 (over z).
Axes of the slice: x: 2, y: 2, z: 4, core: 2. Of those that a mesh axis runs over, the one named last changes fastest.
Arguments:
- grad: bfloat16 [2, 4, 4096, 3072], P('ends', 'dp', 'tp'), may hold values from -1800 to 1800
- master: float32 [4, 1024, 3072], P('tp', ('ends', 'dp')), may hold values from -3 to 3
- moment: float32 [4, 1024, 3072], P('tp', ('ends', 'dp')), may hold values from -3 to 3
- second: float32 [4, 1024, 3072], P('tp', ('ends', 'dp')), may hold values from 0.01 to 1
Outputs:
- weights: bfloat16 [4096, 3072], P('tp')
- master_out: float32 [4, 1024, 3072], P('tp', ('ends', 'dp'))
- moment_out: float32 [4, 1024, 3072], P('tp', ('ends', 'dp'))
- second_out: float32 [4, 1024, 3072], P('tp', ('ends', 'dp'))
All inputs are finite; a program needn't handle non-finite values.
Results may differ from a plain program's by a relative error of at most 0.0034.
Values may be sent and summed in bfloat16 or wider, within the bound.
A program may use at most 128 MiB of HBM per device.

v0:
```python
import functools
import math

import jax
import jax.numpy as jnp
from jax import lax
from jax.experimental import pallas as pl
from jax.experimental.pallas import tpu as pltpu
from jax.sharding import PartitionSpec as P

STEP = 10
MESH = pl.DeviceIdType.MESH
F32 = jnp.float32
BF16 = jnp.bfloat16


def remote(src, dst, send, recv, device):
    return pltpu.make_async_remote_copy(
        src_ref=src, dst_ref=dst, send_sem=send, recv_sem=recv, device_id=device, device_id_type=MESH
    )


def kernel(cfg, grad, master, moment, second, w_out, master_out, moment_out, second_out, *scratch):
    ends, ys, tps, rows, width, pieces, staged = cfg
    if staged:
        w_hbm, (w_out, w_sem), scratch = w_out, scratch[-2:], scratch[:-2]
    (own, peer, part1, land1, part2, land2, total, st0, st1, st2, squares,
     own_sem, st_sem, peer_s, peer_r, s1, r1, s2, r2, ns, nr, a_s, a_r, b_s, b_r, f_s, f_r, p_s, p_r) = scratch
    e, dp, t = lax.axis_index("ends"), lax.axis_index("dp"), lax.axis_index("tp")
    y, c = dp // 2, lax.rem(dp, 2)
    ch = rows // pieces
    devices = ends * ys * 2 * tps
    square = ends == ys
    n1, n2 = (ends, ys) if square else (ys, ends)

    def place(core, da, db):
        if square:
            ends_first = core == 0
            de, dy = jnp.where(ends_first, da, db), jnp.where(ends_first, db, da)
        else:
            de, dy = db, da
        return lax.rem(e + de, ends), lax.rem(y + dy, ys)

    def first_row(core, da, db):
        ee, yy = place(core, da, db)
        return pl.multiple_of(((ee * ys + yy) * 2 + core) * rows, rows)

    def at(da, db):
        ee, yy = place(c, da, db)
        return {"ends": ee, "dp": yy * 2 + c}

    partner = {"dp": y * 2 + (1 - c)}
    shifts1, shifts2 = range(1, n1), range(1, n2)
    order = (
        [(da, db) for da in shifts1 for db in shifts2]
        + [(0, db) for db in shifts2]
        + [(da, 0) for da in shifts1]
        + [(0, 0)]
    )
    slot = lambda da, db: da * n2 + db
    part = lambda k: pl.ds(k * ch, ch)

    def own_copy(da, db, k):
        i = slot(da, db)
        r = pl.multiple_of(first_row(c, da, db) + k * ch, ch)
        return pltpu.make_async_copy(grad.at[pl.ds(r, ch)], own.at[i, part(k)], own_sem.at[i * pieces + k])

    for da, db in order:
        for k in range(pieces):
            own_copy(da, db, k).start()
    state_copies = [
        pltpu.make_async_copy(src, dst, st_sem.at[i])
        for i, (src, dst) in enumerate(((master, st0), (moment, st1), (second, st2)))
    ]

    me = (e * (ys * 2) + dp) * tps + t

    def device_of(i):
        return {"ends": i // (ys * 2 * tps), "dp": lax.rem(i // tps, ys * 2), "tp": lax.rem(i, tps)}

    barrier = pltpu.get_barrier_semaphore()

    @pl.loop(1, devices)
    def _(d):
        pl.semaphore_signal(barrier, inc=1, device_id=device_of(lax.rem(me + d, devices)), device_id_type=MESH)

    pl.semaphore_wait(barrier, devices - 1)

    for da, db in order:
        for k in range(pieces):
            i = slot(da, db)
            r = pl.multiple_of(first_row(1 - c, da, db) + k * ch, ch)
            remote(grad.at[pl.ds(r, ch)], peer.at[i, part(k)], peer_s, peer_r.at[i * pieces + k], partner).start()
    for copy in state_copies:
        copy.start()

    def chip_sum(da, db, k):
        i = slot(da, db)
        own_copy(da, db, k).wait()
        remote(peer.at[i, part(k)], peer.at[i, part(k)], peer_s, peer_r.at[i * pieces + k], partner).wait_recv()
        return own[i, part(k), :].astype(F32) + peer[i, part(k), :].astype(F32)

    def copy1(da, db, k):
        i = (da - 1) * n2 + db
        return remote(part1.at[i, part(k)], land1.at[i, part(k)], s1, r1.at[i * pieces + k], at(da, 0))

    def copy2(db, k):
        i = db - 1
        return remote(part2.at[i, part(k)], land2.at[i, part(k)], s2, r2.at[i * pieces + k], at(0, db))

    def send1(da, db, k):
        part1[(da - 1) * n2 + db, part(k), :] = chip_sum(da, db, k).astype(BF16)
        copy1(da, db, k).start()

    def sum1(db, k):
        value = chip_sum(0, db, k)
        for da in shifts1:
            copy1(da, db, k).wait_recv()
            value = value + land1[(da - 1) * n2 + db, part(k), :].astype(F32)
        return value

    for k in range(pieces):
        for da in shifts1:
            for db in shifts2:
                send1(da, db, k)
    for k in range(pieces):
        for da in shifts1:
            send1(da, 0, k)
        for db in shifts2:
            part2[db - 1, part(k), :] = sum1(db, k).astype(BF16)
            copy2(db, k).start()
    acc = jnp.zeros((8, width), F32)
    for k in range(pieces):
        value = sum1(0, k)
        for db in shifts2:
            copy2(db, k).wait_recv()
            value = value + land2[db - 1, part(k), :].astype(F32)
        total[part(k), :] = value
        value = value * value
        for r in range(0, ch, 8):
            acc = acc + value[r : r + 8, :]

    mine = acc[:, :128]
    for j in range(128, width, 128):
        mine = mine + acc[:, j : j + 128]
    squares[me] = jnp.sum(mine, axis=0, keepdims=True)

    @pl.loop(1, devices)
    def _(d):
        remote(squares.at[me], squares.at[me], ns, nr, device_of(lax.rem(me + d, devices))).start()

    others = squares.at[pl.ds(0, devices - 1)]
    everyone = remote(others, others, ns, nr, partner)
    for copy in state_copies:
        copy.wait()
    everyone.wait_recv()
    everyone.wait_send()
    norm2 = jnp.full((8, 128), jnp.sum(jnp.sum(squares[...], axis=0)), F32)
    entries = float(tps * ends * ys * 2 * rows * width)
    factor = jnp.minimum(F32(1.0), F32(math.sqrt(entries)) / (jnp.sqrt(norm2) + 1e-06))[:1, :1]

    my_row = first_row(c, 0, 0)

    def piece_of(da, db, k):
        return w_out.at[pl.ds(pl.multiple_of(first_row(c, da, db) + k * ch, ch), ch)]

    def copy_a(da, src, k):
        return remote(src, src, a_s, a_r.at[(da - 1) * pieces + k], at(da, 0))

    def copy_b(db, src, k):
        return remote(src, src, b_s, b_r.at[(db - 1) * pieces + k], at(0, db))

    def copy_f(da, db, src, k):
        return remote(src, src, f_s, f_r.at[((da - 1) * (n2 - 1) + db - 1) * pieces + k], at(0, db))

    def copy_p(src):
        return remote(src, src, p_s, p_r, partner)

    for k in range(pieces):
        @pl.loop(0, ch // 16)
        def _(g):
            at_row = pl.multiple_of(k * ch + g * 16, 16)
            here = pl.ds(at_row, 16)
            clipped = factor * total[here, :]
            m = 0.9 * st1[here, :] + 0.1 * clipped
            v = 0.999 * st2[here, :] + 0.001 * clipped * clipped
            update = m / (1.0 - 0.9**STEP) / (jnp.sqrt(v / (1.0 - 0.999**STEP)) + 1e-08)
            w = st0[here, :]
            w = w - 0.01 * (update + 0.1 * w)
            moment_out[here, :] = m
            second_out[here, :] = v
            master_out[here, :] = w
            w_out[pl.ds(pl.multiple_of(my_row + at_row, 16), 16), :] = w.astype(BF16)

        src = piece_of(0, 0, k)
        for da in shifts1:
            copy_a(da, src, k).start()
        for db in shifts2:
            copy_b(db, src, k).start()
        copy_p(src).start()

    for k in range(pieces):
        for da in shifts1:
            src = piece_of(n1 - da, 0, k)
            copy_a(da, src, k).wait_recv()
            for db in shifts2:
                copy_f(da, db, src, k).start()
            copy_p(src).start()
        for db in shifts2:
            src = piece_of(0, n2 - db, k)
            copy_b(db, src, k).wait_recv()
            copy_p(src).start()
    for k in range(pieces):
        for da in shifts1:
            for db in shifts2:
                src = piece_of(n1 - da, n2 - db, k)
                copy_f(da, db, src, k).wait_recv()
                copy_p(src).start()

    half = w_out.at[pl.ds(0, n1 * n2 * rows)]
    remote(half, half, p_s, p_r, partner).wait_recv()
    remote(half, half, p_s, p_r, partner).wait_send()
    remote(peer, peer, peer_s, peer_r.at[0], partner).wait_send()
    remote(part1, land1, s1, r1.at[0], partner).wait_send()
    remote(part2, land2, s2, r2.at[0], partner).wait_send()
    for sem, count, recv in ((a_s, n1 - 1, a_r), (b_s, n2 - 1, b_r), (f_s, (n1 - 1) * (n2 - 1), f_r)):
        ref = w_out.at[pl.ds(0, count * rows)]
        remote(ref, ref, sem, recv.at[0], partner).wait_send()
    if staged:
        final = pltpu.make_async_copy(w_out, w_hbm, w_sem)
        final.start()
        final.wait()


def put_out(*refs):
    count = len(refs) // 2
    sems = refs[-1]
    copies = [
        pltpu.make_async_copy(src, dst, sems.at[i])
        for i, (src, dst) in enumerate(zip(refs[:count], refs[count : 2 * count]))
    ]
    for copy in copies:
        copy.start()
    for copy in copies:
        copy.wait()


def per_device(mesh, grad, master, moment, second):
    ends, dps, tps = (mesh.shape[name] for name in ("ends", "dp", "tp"))
    ys = dps // 2
    rows_tp, width = grad.shape[2:]
    rows = rows_tp // (ends * dps)
    pieces = 4 if rows % 64 == 0 else 1
    n1, n2 = (ends, ys) if ends == ys else (ys, ends)
    blocks = n1 * n2
    devices = ends * dps * tps
    dma = lambda n: pltpu.SemaphoreType.DMA((n,))
    one = pltpu.SemaphoreType.DMA
    block = lambda n, dtype=BF16: pltpu.VMEM((n, rows, width), dtype)
    state = lambda: pltpu.VMEM((rows, width), F32)
    scratch = [
        block(blocks), block(blocks),
        block((n1 - 1) * n2), block((n1 - 1) * n2),
        block(n2 - 1), block(n2 - 1),
        state(), state(), state(), state(),
        pltpu.VMEM((devices, 1, 128), F32),
        dma(blocks * pieces), dma(3), one, dma(blocks * pieces),
        one, dma((n1 - 1) * n2 * pieces), one, dma((n2 - 1) * pieces),
        one, one,
        one, dma((n1 - 1) * pieces), one, dma((n2 - 1) * pieces),
        one, dma((n1 - 1) * (n2 - 1) * pieces),
        one, one,
    ]
    block_bytes = rows * width * 2
    staged = rows_tp * width * 2 > 8 << 20
    if staged:
        scratch += [pltpu.VMEM((rows_tp, width), BF16), one]
    limit = block_bytes * (2 * blocks + 2 * (n1 - 1) * n2 + 2 * (n2 - 1) + 8 + staged * ends * dps) + devices * 4096 + (3 << 20)
    stays = pl.BlockSpec(memory_space=pltpu.HBM)
    vmem = pl.BlockSpec(memory_space=pltpu.VMEM)
    vmem_any = pl.BlockSpec(memory_space=pl.ANY)
    results = pl.pallas_call(
        functools.partial(kernel, (ends, ys, tps, rows, width, pieces, staged)),
        out_shape=(
            (pltpu.HBM if staged else pltpu.VMEM)((rows_tp, width), BF16),
            pltpu.VMEM((rows, width), F32),
            pltpu.VMEM((rows, width), F32),
            pltpu.VMEM((rows, width), F32),
        ),
        in_specs=[stays] * 4,
        out_specs=(stays if staged else vmem,) + (vmem,) * 3,
        scratch_shapes=scratch,
        compiler_params=pltpu.CompilerParams(collective_id=0, has_side_effects=True, vmem_limit_bytes=limit),
        name="sum_update_gather",
    )(*(pltpu.with_memory_space_constraint(x, pltpu.HBM) for x in (grad[0, 0], master[0], moment[0], second[0])))
    first = 1 if staged else 0
    here = results[first:]
    out = pl.pallas_call(
        put_out,
        out_shape=tuple(pltpu.HBM(x.shape, x.dtype) for x in here),
        in_specs=[vmem_any] * len(here),
        out_specs=(stays,) * len(here),
        scratch_shapes=[dma(len(here))],
        compiler_params=pltpu.CompilerParams(vmem_limit_bytes=1 << 20),
        name="put_out",
    )(*(pltpu.with_memory_space_constraint(x, pltpu.VMEM) for x in here))
    weights, master_out, moment_out, second_out = tuple(results[:first]) + tuple(out)
    return (weights, master_out[None], moment_out[None], second_out[None])


def solution(mesh):
    rows = P("tp", ("ends", "dp"), None)
    return jax.shard_map(
        functools.partial(per_device, mesh),
        mesh=mesh,
        in_specs=(P("ends", "dp", "tp", None), rows, rows, rows),
        out_specs=(P("tp", None), rows, rows, rows),
        check_vma=False,
    )
```

profile of v0, /device:TPU:0, one launch (start us, length us, event | category | flops | bytes accessed | tf_op | source)
XLA Modules:
  0.0 74.4 jit_solution(10207252818062011786)
XLA Ops:
  0.6 69.6 %sum_update_gather.1 = (bf16[1024,3072]{1,0:T(8,128)(2,1)S(1)}, f32[128,3072]{1,0:T(8,128)S(1)}, f32[128,3072]{1,0:T(8,128)S(1)}, f32[128,3072]{1,0:T(8,128)S(1)}) custom-call(bf16[1024,3072]{1,0:T(8,128)(2,1)} %bitcast.7, f32[128,3072]{1,0:T(8,128)} %bitcast.8, f32[128,3072]{1,0:T(8,128)} %bitcast.9, f32[128,3072]{1,0:T(8,128)} %bitcast.10), custom_call_target="tpu_custom_call" | custom-call | tf_op jit(solution)/shard_map/sum_update_gather/pallas_call | solution.py:282
  70.2 4.2 %put_out.1 = (bf16[1024,3072]{1,0:T(8,128)(2,1)}, f32[128,3072]{1,0:T(8,128)}, f32[128,3072]{1,0:T(8,128)}, f32[128,3072]{1,0:T(8,128)}) custom-call(bf16[1024,3072]{1,0:T(8,128)(2,1)S(1)} %get-tuple-element.12.refs_0_, f32[128,3072]{1,0:T(8,128)S(1)} %get-tuple-element.13.refs_1_, f32[128,3072]{1,0:T(8,128)S(1)} %get-tuple-element.14.refs_2_, ...), custom_call_target="tpu_custom_call" | custom-call | tf_op jit(solution)/shard_map/put_out/pallas_call | solution.py:298
where the time goes:
time: 74.6 us; the launch traced here: 74.4 us
  Pallas kernels  73.8 us (99%)
    pallas_call x1, Pallas kernels, per_device(): pl.pallas_call(functools.partial(kernel, (ends, ys, tps, rows, width, pie...  69.6 us
    pallas_call x1, Pallas kernels, per_device(): pl.pallas_call(put_out, out_shape=tuple((pltpu.HBM(x.shape, x.dtype) for...  4.2 us

commit v1 on v0

--- a/solution.py
+++ b/solution.py
@@ -21,14 +21,15 @@
 
 
 def kernel(cfg, grad, master, moment, second, w_out, master_out, moment_out, second_out, *scratch):
-    ends, ys, tps, rows, width, pieces, staged = cfg
+    ends, ys, tps, rows, width, cuts, staged = cfg
     if staged:
         w_hbm, (w_out, w_sem), scratch = w_out, scratch[-2:], scratch[:-2]
     (own, peer, part1, land1, part2, land2, total, st0, st1, st2, squares,
-     own_sem, st_sem, peer_s, peer_r, s1, r1, s2, r2, ns, nr, a_s, a_r, b_s, b_r, f_s, f_r, p_s, p_r) = scratch
+     own_sem, st_sem, peer_s, peer_r, s1, r1, s2, r2, ns, nr, a_s, a_r, b_s, b_r, f_s, f_r, p_s, p_r,
+     up, down, here_p, here_1, here_2) = scratch
     e, dp, t = lax.axis_index("ends"), lax.axis_index("dp"), lax.axis_index("tp")
     y, c = dp // 2, lax.rem(dp, 2)
-    ch = rows // pieces
+    pieces = len(cuts)
     devices = ends * ys * 2 * tps
     square = ends == ys
     n1, n2 = (ends, ys) if square else (ys, ends)
@@ -58,12 +59,27 @@
         + [(0, 0)]
     )
     slot = lambda da, db: da * n2 + db
-    part = lambda k: pl.ds(k * ch, ch)
+    part = lambda k: pl.ds(*cuts[k])
+
+    me = (e * (ys * 2) + dp) * tps + t
+    barrier = pltpu.get_barrier_semaphore()
+    signal = lambda sem, device: pl.semaphore_signal(sem, inc=1, device_id=device, device_id_type=MESH)
+    planes = [at(da, 0) for da in shifts1], [at(0, db) for db in shifts2]
+    above, below = {"tp": t + 1}, {"tp": t - 1}
+    has_above, has_below = t < tps - 1, t > 0
+
+    for device in planes[0] + planes[1] + [partner]:
+        signal(barrier, device)
+    pl.when(has_above)(lambda: signal(barrier, above))
+    pl.when(has_below)(lambda: signal(barrier, below))
+
+    def rows_at(start, k):
+        first, size = cuts[k]
+        return pl.ds(pl.multiple_of(start + first, 16), size)
 
     def own_copy(da, db, k):
         i = slot(da, db)
-        r = pl.multiple_of(first_row(c, da, db) + k * ch, ch)
-        return pltpu.make_async_copy(grad.at[pl.ds(r, ch)], own.at[i, part(k)], own_sem.at[i * pieces + k])
+        return pltpu.make_async_copy(grad.at[rows_at(first_row(c, da, db), k)], own.at[i, part(k)], own_sem.at[i * pieces + k])
 
     for da, db in order:
         for k in range(pieces):
@@ -72,27 +88,39 @@
         pltpu.make_async_copy(src, dst, st_sem.at[i])
         for i, (src, dst) in enumerate(((master, st0), (moment, st1), (second, st2)))
     ]
-
-    me = (e * (ys * 2) + dp) * tps + t
-
-    def device_of(i):
-        return {"ends": i // (ys * 2 * tps), "dp": lax.rem(i // tps, ys * 2), "tp": lax.rem(i, tps)}
-
-    barrier = pltpu.get_barrier_semaphore()
-
-    @pl.loop(1, devices)
-    def _(d):
-        pl.semaphore_signal(barrier, inc=1, device_id=device_of(lax.rem(me + d, devices)), device_id_type=MESH)
-
-    pl.semaphore_wait(barrier, devices - 1)
+    pl.semaphore_wait(barrier, n1 + n2 - 1 + has_above.astype(jnp.int32) + has_below.astype(jnp.int32))
 
     for da, db in order:
         for k in range(pieces):
             i = slot(da, db)
-            r = pl.multiple_of(first_row(1 - c, da, db) + k * ch, ch)
-            remote(grad.at[pl.ds(r, ch)], peer.at[i, part(k)], peer_s, peer_r.at[i * pieces + k], partner).start()
+            remote(grad.at[rows_at(first_row(1 - c, da, db), k)], peer.at[i, part(k)], peer_s, peer_r.at[i * pieces + k], partner).start()
     for copy in state_copies:
         copy.start()
+    pl.when(jnp.logical_and(has_above, t == 0))(lambda: signal(up, above))
+    pl.when(jnp.logical_and(has_below, t == tps - 1))(lambda: signal(down, below))
+
+    def meet(step):
+        if step == 0:
+            @pl.when(has_below)
+            def _():
+                pl.semaphore_wait(up, 1)
+                pl.when(has_above)(lambda: signal(up, above))
+        if step == 1:
+            @pl.when(has_above)
+            def _():
+                pl.semaphore_wait(down, 1)
+                pl.when(has_below)(lambda: signal(down, below))
+            signal(here_p, partner)
+        if step == 2:
+            pl.semaphore_wait(here_p, 1)
+            for device in planes[0]:
+                signal(here_1, device)
+        if step == 3:
+            pl.semaphore_wait(here_1, n1 - 1)
+            for device in planes[1]:
+                signal(here_2, device)
+        if step == 4:
+            pl.semaphore_wait(here_2, n2 - 1)
 
     def chip_sum(da, db, k):
         i = slot(da, db)
@@ -129,6 +157,11 @@
         for db in shifts2:
             part2[db - 1, part(k), :] = sum1(db, k).astype(BF16)
             copy2(db, k).start()
+        if k < 3:
+            meet(k)
+    for step in range(min(pieces, 3), 4):
+        meet(step)
+    meet(4)
     acc = jnp.zeros((8, width), F32)
     for k in range(pieces):
         value = sum1(0, k)
@@ -137,7 +170,7 @@
             value = value + land2[db - 1, part(k), :].astype(F32)
         total[part(k), :] = value
         value = value * value
-        for r in range(0, ch, 8):
+        for r in range(0, cuts[k][1], 8):
             acc = acc + value[r : r + 8, :]
 
     mine = acc[:, :128]
@@ -145,9 +178,18 @@
         mine = mine + acc[:, j : j + 128]
     squares[me] = jnp.sum(mine, axis=0, keepdims=True)
 
-    @pl.loop(1, devices)
-    def _(d):
-        remote(squares.at[me], squares.at[me], ns, nr, device_of(lax.rem(me + d, devices))).start()
+    high = t >= tps // 2
+    for j in range(tps - 1):
+        up_from, down_from = j + (t <= j).astype(jnp.int32), tps - 1 - j - (t >= tps - 1 - j).astype(jnp.int32)
+        for de in range(ends):
+            for ddp in range(ys * 2):
+                device = {"ends": lax.rem(e + de, ends), "dp": lax.rem(dp + ddp, ys * 2), "tp": jnp.where(high, up_from, down_from)}
+                remote(squares.at[me], squares.at[me], ns, nr, device).start()
+    for de in range(ends):
+        for ddp in range(ys * 2):
+            if de or ddp:
+                device = {"ends": lax.rem(e + de, ends), "dp": lax.rem(dp + ddp, ys * 2)}
+                remote(squares.at[me], squares.at[me], ns, nr, device).start()
 
     others = squares.at[pl.ds(0, devices - 1)]
     everyone = remote(others, others, ns, nr, partner)
@@ -162,7 +204,7 @@
     my_row = first_row(c, 0, 0)
 
     def piece_of(da, db, k):
-        return w_out.at[pl.ds(pl.multiple_of(first_row(c, da, db) + k * ch, ch), ch)]
+        return w_out.at[rows_at(first_row(c, da, db), k)]
 
     def copy_a(da, src, k):
         return remote(src, src, a_s, a_r.at[(da - 1) * pieces + k], at(da, 0))
@@ -177,9 +219,9 @@
         return remote(src, src, p_s, p_r, partner)
 
     for k in range(pieces):
-        @pl.loop(0, ch // 16)
+        @pl.loop(0, cuts[k][1] // 16)
         def _(g):
-            at_row = pl.multiple_of(k * ch + g * 16, 16)
+            at_row = pl.multiple_of(cuts[k][0] + g * 16, 16)
             here = pl.ds(at_row, 16)
             clipped = factor * total[here, :]
             m = 0.9 * st1[here, :] + 0.1 * clipped
@@ -250,12 +292,15 @@
     ys = dps // 2
     rows_tp, width = grad.shape[2:]
     rows = rows_tp // (ends * dps)
-    pieces = 4 if rows % 64 == 0 else 1
+    sizes = [16] + [32] * (rows // 32 - 1) + [16] if rows % 32 == 0 and rows >= 64 else [rows]
+    cuts = tuple((sum(sizes[:k]), size) for k, size in enumerate(sizes))
+    pieces = len(cuts)
     n1, n2 = (ends, ys) if ends == ys else (ys, ends)
     blocks = n1 * n2
     devices = ends * dps * tps
     dma = lambda n: pltpu.SemaphoreType.DMA((n,))
     one = pltpu.SemaphoreType.DMA
+    regular = pltpu.SemaphoreType.REGULAR
     block = lambda n, dtype=BF16: pltpu.VMEM((n, rows, width), dtype)
     state = lambda: pltpu.VMEM((rows, width), F32)
     scratch = [
@@ -270,6 +315,7 @@
         one, dma((n1 - 1) * pieces), one, dma((n2 - 1) * pieces),
         one, dma((n1 - 1) * (n2 - 1) * pieces),
         one, one,
+        regular, regular, regular, regular, regular,
     ]
     block_bytes = rows * width * 2
     staged = rows_tp * width * 2 > 8 << 20
@@ -280,7 +326,7 @@
     vmem = pl.BlockSpec(memory_space=pltpu.VMEM)
     vmem_any = pl.BlockSpec(memory_space=pl.ANY)
     results = pl.pallas_call(
-        functools.partial(kernel, (ends, ys, tps, rows, width, pieces, staged)),
+        functools.partial(kernel, (ends, ys, tps, rows, width, cuts, staged)),
         out_shape=(
             (pltpu.HBM if staged else pltpu.VMEM)((rows_tp, width), BF16),
             pltpu.VMEM((rows, width), F32),

time: 74.6 us -> 71.8 us (0.962)
  Pallas kernels: 73.8 us -> 71 us
    pallas_call x1, Pallas kernels: 69.6 us -> 66.8 us  [per_device(): pl.pallas_call(functools.partial(kernel, (ends, ys, tps, rows, width, cut...]
where the time goes in v1:
time: 71.8 us; the launch traced here: 71.7 us
  Pallas kernels  71 us (99%)
    pallas_call x1, Pallas kernels, per_device(): pl.pallas_call(functools.partial(kernel, (ends, ys, tps, rows, width, cut...  66.8 us
    pallas_call x1, Pallas kernels, per_device(): pl.pallas_call(put_out, out_shape=tuple((pltpu.HBM(x.shape, x.dtype) for...  4.2 us

profile of v1, /device:TPU:0, one launch (start us, length us, event | category | flops | bytes accessed | tf_op | source)
XLA Modules:
  0.0 71.7 jit_solution(11829980871696806719)
XLA Ops:
  0.6 66.8 %sum_update_gather.1 = (bf16[1024,3072]{1,0:T(8,128)(2,1)S(1)}, f32[128,3072]{1,0:T(8,128)S(1)}, f32[128,3072]{1,0:T(8,128)S(1)}, f32[128,3072]{1,0:T(8,128)S(1)}) custom-call(bf16[1024,3072]{1,0:T(8,128)(2,1)} %bitcast.7, f32[128,3072]{1,0:T(8,128)} %bitcast.8, f32[128,3072]{1,0:T(8,128)} %bitcast.9, f32[128,3072]{1,0:T(8,128)} %bitcast.10), custom_call_target="tpu_custom_call" | custom-call | tf_op jit(solution)/shard_map/sum_update_gather/pallas_call | solution.py:328
  67.5 4.2 %put_out.1 = (bf16[1024,3072]{1,0:T(8,128)(2,1)}, f32[128,3072]{1,0:T(8,128)}, f32[128,3072]{1,0:T(8,128)}, f32[128,3072]{1,0:T(8,128)}) custom-call(bf16[1024,3072]{1,0:T(8,128)(2,1)S(1)} %get-tuple-element.12.refs_0_, f32[128,3072]{1,0:T(8,128)S(1)} %get-tuple-element.13.refs_1_, f32[128,3072]{1,0:T(8,128)S(1)} %get-tuple-element.14.refs_2_, ...), custom_call_target="tpu_custom_call" | custom-call | tf_op jit(solution)/shard_map/put_out/pallas_call | solution.py:344

commit v2 on v1

--- a/solution.py
+++ b/solution.py
@@ -12,6 +12,7 @@
 MESH = pl.DeviceIdType.MESH
 F32 = jnp.float32
 BF16 = jnp.bfloat16
+EARLY = 4
 
 
 def remote(src, dst, send, recv, device):
@@ -21,11 +22,11 @@
 
 
 def kernel(cfg, grad, master, moment, second, w_out, master_out, moment_out, second_out, *scratch):
-    ends, ys, tps, rows, width, cuts, staged = cfg
+    ends, ys, tps, rows, width, cuts, early, staged = cfg
     if staged:
         w_hbm, (w_out, w_sem), scratch = w_out, scratch[-2:], scratch[:-2]
-    (own, peer, part1, land1, part2, land2, total, st0, st1, st2, squares,
-     own_sem, st_sem, peer_s, peer_r, s1, r1, s2, r2, ns, nr, a_s, a_r, b_s, b_r, f_s, f_r, p_s, p_r,
+    (own, peer, part1, land1, part2, land2, total, states, squares, terms,
+     own_sem, st_sem, peer_s, peer_r, s1, s2, recv, ns, nr, q_s, q_r, qp_r, g_s, g_r, h_s, h_r,
      up, down, here_p, here_1, here_2) = scratch
     e, dp, t = lax.axis_index("ends"), lax.axis_index("dp"), lax.axis_index("tp")
     y, c = dp // 2, lax.rem(dp, 2)
@@ -33,6 +34,8 @@
     devices = ends * ys * 2 * tps
     square = ends == ys
     n1, n2 = (ends, ys) if square else (ys, ends)
+    blocks = n1 * n2
+    first = cuts[0][1]
 
     def place(core, da, db):
         if square:
@@ -42,9 +45,12 @@
             de, dy = db, da
         return lax.rem(e + de, ends), lax.rem(y + dy, ys)
 
+    def member(core, da, db):
+        ee, yy = place(core, da, db)
+        return (ee * ys + yy) * 2 + core
+
     def first_row(core, da, db):
-        ee, yy = place(core, da, db)
-        return pl.multiple_of(((ee * ys + yy) * 2 + core) * rows, rows)
+        return pl.multiple_of(member(core, da, db) * rows, rows)
 
     def at(da, db):
         ee, yy = place(c, da, db)
@@ -52,12 +58,8 @@
 
     partner = {"dp": y * 2 + (1 - c)}
     shifts1, shifts2 = range(1, n1), range(1, n2)
-    order = (
-        [(da, db) for da in shifts1 for db in shifts2]
-        + [(0, db) for db in shifts2]
-        + [(da, 0) for da in shifts1]
-        + [(0, 0)]
-    )
+    corners = [(da, db) for da in shifts1 for db in shifts2]
+    order = corners + [(0, db) for db in shifts2] + [(da, 0) for da in shifts1] + [(0, 0)]
     slot = lambda da, db: da * n2 + db
     part = lambda k: pl.ds(*cuts[k])
 
@@ -74,26 +76,33 @@
     pl.when(has_below)(lambda: signal(barrier, below))
 
     def rows_at(start, k):
-        first, size = cuts[k]
-        return pl.ds(pl.multiple_of(start + first, 16), size)
-
-    def own_copy(da, db, k):
+        at_row, size = cuts[k]
+        return pl.ds(pl.multiple_of(start + at_row, 16), size)
+
+    def own_copy(da, db):
         i = slot(da, db)
-        return pltpu.make_async_copy(grad.at[rows_at(first_row(c, da, db), k)], own.at[i, part(k)], own_sem.at[i * pieces + k])
+        return pltpu.make_async_copy(grad.at[pl.ds(first_row(c, da, db), rows)], own.at[i], own_sem.at[i])
 
     for da, db in order:
-        for k in range(pieces):
-            own_copy(da, db, k).start()
+        own_copy(da, db).start()
     state_copies = [
-        pltpu.make_async_copy(src, dst, st_sem.at[i])
-        for i, (src, dst) in enumerate(((master, st0), (moment, st1), (second, st2)))
+        pltpu.make_async_copy(src, states.at[i], st_sem.at[i]) for i, src in enumerate((master, moment, second))
     ]
     pl.semaphore_wait(barrier, n1 + n2 - 1 + has_above.astype(jnp.int32) + has_below.astype(jnp.int32))
 
+    def peer_copy(da, db, k):
+        i, start = slot(da, db), first_row(1 - c, da, db)
+        if da and db:
+            sem = peer_r.at[corners.index((da, db)) * pieces + k]
+            return remote(grad.at[rows_at(start, k)], peer.at[i, part(k)], peer_s, sem, partner)
+        sem = peer_r.at[len(corners) * pieces + order.index((da, db)) - len(corners)]
+        return remote(grad.at[pl.ds(start, rows)], peer.at[i], peer_s, sem, partner)
+
+    cut = lambda da, db: pieces if da and db else 1
+
     for da, db in order:
-        for k in range(pieces):
-            i = slot(da, db)
-            remote(grad.at[rows_at(first_row(1 - c, da, db), k)], peer.at[i, part(k)], peer_s, peer_r.at[i * pieces + k], partner).start()
+        for k in range(cut(da, db)):
+            peer_copy(da, db, k).start()
     for copy in state_copies:
         copy.start()
     pl.when(jnp.logical_and(has_above, t == 0))(lambda: signal(up, above))
@@ -124,17 +133,19 @@
 
     def chip_sum(da, db, k):
         i = slot(da, db)
-        own_copy(da, db, k).wait()
-        remote(peer.at[i, part(k)], peer.at[i, part(k)], peer_s, peer_r.at[i * pieces + k], partner).wait_recv()
+        if k == 0:
+            own_copy(da, db).wait()
+        if k < cut(da, db):
+            peer_copy(da, db, k).wait_recv()
         return own[i, part(k), :].astype(F32) + peer[i, part(k), :].astype(F32)
 
     def copy1(da, db, k):
         i = (da - 1) * n2 + db
-        return remote(part1.at[i, part(k)], land1.at[i, part(k)], s1, r1.at[i * pieces + k], at(da, 0))
+        return remote(part1.at[i, part(k)], land1.at[i, part(k)], s1, recv.at[i * pieces + k], at(da, 0))
 
     def copy2(db, k):
         i = db - 1
-        return remote(part2.at[i, part(k)], land2.at[i, part(k)], s2, r2.at[i * pieces + k], at(0, db))
+        return remote(part2.at[i, part(k)], land2.at[i, part(k)], s2, recv.at[((n1 - 1) * n2 + i) * pieces + k], at(0, db))
 
     def send1(da, db, k):
         part1[(da - 1) * n2 + db, part(k), :] = chip_sum(da, db, k).astype(BF16)
@@ -161,6 +172,11 @@
             meet(k)
     for step in range(min(pieces, 3), 4):
         meet(step)
+    for copy in state_copies:
+        copy.wait()
+    mine = member(c, 0, 0)
+    for i in range(3):
+        terms[mine, i] = states[i, pl.ds(0, first), pl.ds(0, early)].astype(BF16)
     meet(4)
     acc = jnp.zeros((8, width), F32)
     for k in range(pieces):
@@ -169,14 +185,16 @@
             copy2(db, k).wait_recv()
             value = value + land2[db - 1, part(k), :].astype(F32)
         total[part(k), :] = value
+        if k == 0:
+            terms[mine, 3] = value[:, :early].astype(BF16)
         value = value * value
         for r in range(0, cuts[k][1], 8):
             acc = acc + value[r : r + 8, :]
 
-    mine = acc[:, :128]
+    lanes = acc[:, :128]
     for j in range(128, width, 128):
-        mine = mine + acc[:, j : j + 128]
-    squares[me] = jnp.sum(mine, axis=0, keepdims=True)
+        lanes = lanes + acc[:, j : j + 128]
+    squares[me] = jnp.sum(lanes, axis=0, keepdims=True)
 
     high = t >= tps // 2
     for j in range(tps - 1):
@@ -191,83 +209,132 @@
                 device = {"ends": lax.rem(e + de, ends), "dp": lax.rem(dp + ddp, ys * 2)}
                 remote(squares.at[me], squares.at[me], ns, nr, device).start()
 
+    class Gather:
+        def __init__(self, src, count, send, sems, send_p, recv_p):
+            self.src, self.count, self.sems, self.send, self.send_p, self.recv_p = src, count, sems, send, send_p, recv_p
+
+        def copy(self, i, da, db, k, device):
+            ref = self.src(da, db, k)
+            return remote(ref, ref, self.send(k), self.sems.at[i * self.count + k], device)
+
+        def a(self, da, from_da, k):
+            return self.copy(da - 1, from_da, 0, k, at(da, 0))
+
+        def b(self, db, from_db, k):
+            return self.copy(n1 - 2 + db, 0, from_db, k, at(0, db))
+
+        def f(self, da, db, from_da, from_db, k):
+            return self.copy(n1 + n2 - 2 + (da - 1) * (n2 - 1) + db - 1, from_da, from_db, k, at(0, db))
+
+        def p(self, da, db, k):
+            ref = self.src(da, db, k)
+            remote(ref, ref, self.send_p(k), self.recv_p(k), partner).start()
+
+        def own(self, k):
+            for da in shifts1:
+                self.a(da, 0, k).start()
+            for db in shifts2:
+                self.b(db, 0, k).start()
+            self.p(0, 0, k)
+
+        def forward(self, k):
+            for da in shifts1:
+                self.a(da, n1 - da, k).wait_recv()
+                for db in shifts2:
+                    self.f(da, db, n1 - da, 0, k).start()
+                self.p(n1 - da, 0, k)
+            for db in shifts2:
+                self.b(db, n2 - db, k).wait_recv()
+                self.p(0, n2 - db, k)
+
+        def last(self, k):
+            for da in shifts1:
+                for db in shifts2:
+                    self.f(da, db, n1 - da, n2 - db, k).wait_recv()
+                    self.p(n1 - da, n2 - db, k)
+
+    halves = 2
+    quarter = lambda da, db, k: terms.at[member(c, da, db), pl.ds(4 // halves * k, 4 // halves)]
+    ahead = Gather(quarter, halves, lambda k: q_s, q_r, lambda k: q_s, lambda k: qp_r)
+
+    def piece_of(da, db, k):
+        here = rows_at(first_row(c, da, db), k)
+        return w_out.at[here, pl.ds(early, width - early)] if k == 0 else w_out.at[here]
+
+    gather = Gather(piece_of, pieces, lambda k: g_s if k else h_s, recv, lambda k: g_s if k else h_s, lambda k: g_r if k else h_r)
+
+    for k in range(halves):
+        ahead.own(k)
+    for k in range(halves):
+        ahead.forward(k)
+    remote(peer, peer, peer_s, peer_r.at[0], partner).wait_send()
+    remote(part1, land1, s1, recv.at[0], partner).wait_send()
+    remote(part2, land2, s2, recv.at[0], partner).wait_send()
+
     others = squares.at[pl.ds(0, devices - 1)]
     everyone = remote(others, others, ns, nr, partner)
-    for copy in state_copies:
-        copy.wait()
     everyone.wait_recv()
-    everyone.wait_send()
     norm2 = jnp.full((8, 128), jnp.sum(jnp.sum(squares[...], axis=0)), F32)
     entries = float(tps * ends * ys * 2 * rows * width)
     factor = jnp.minimum(F32(1.0), F32(math.sqrt(entries)) / (jnp.sqrt(norm2) + 1e-06))[:1, :1]
 
+    def adam(w, m, v, s):
+        clipped = factor * s
+        m = 0.9 * m + 0.1 * clipped
+        v = 0.999 * v + 0.001 * clipped * clipped
+        update = m / (1.0 - 0.9**STEP) / (jnp.sqrt(v / (1.0 - 0.999**STEP)) + 1e-08)
+        return w - 0.01 * (update + 0.1 * w), m, v
+
     my_row = first_row(c, 0, 0)
 
-    def piece_of(da, db, k):
-        return w_out.at[rows_at(first_row(c, da, db), k)]
-
-    def copy_a(da, src, k):
-        return remote(src, src, a_s, a_r.at[(da - 1) * pieces + k], at(da, 0))
-
-    def copy_b(db, src, k):
-        return remote(src, src, b_s, b_r.at[(db - 1) * pieces + k], at(0, db))
-
-    def copy_f(da, db, src, k):
-        return remote(src, src, f_s, f_r.at[((da - 1) * (n2 - 1) + db - 1) * pieces + k], at(0, db))
-
-    def copy_p(src):
-        return remote(src, src, p_s, p_r, partner)
-
-    for k in range(pieces):
+    def step(at_row, size, columns, weights):
+        here = pl.ds(at_row, size)
+        w, m, v = adam(states[0, here, columns], states[1, here, columns], states[2, here, columns], total[here, columns])
+        moment_out[here, columns] = m
+        second_out[here, columns] = v
+        master_out[here, columns] = w
+        if weights:
+            w_out[pl.ds(pl.multiple_of(my_row + at_row, 16), size), columns] = w.astype(BF16)
+
+    step(0, first, pl.ds(early, width - early), True)
+    gather.own(0)
+    for k in range(1, pieces):
         @pl.loop(0, cuts[k][1] // 16)
         def _(g):
-            at_row = pl.multiple_of(cuts[k][0] + g * 16, 16)
-            here = pl.ds(at_row, 16)
-            clipped = factor * total[here, :]
-            m = 0.9 * st1[here, :] + 0.1 * clipped
-            v = 0.999 * st2[here, :] + 0.001 * clipped * clipped
-            update = m / (1.0 - 0.9**STEP) / (jnp.sqrt(v / (1.0 - 0.999**STEP)) + 1e-08)
-            w = st0[here, :]
-            w = w - 0.01 * (update + 0.1 * w)
-            moment_out[here, :] = m
-            second_out[here, :] = v
-            master_out[here, :] = w
-            w_out[pl.ds(pl.multiple_of(my_row + at_row, 16), 16), :] = w.astype(BF16)
-
-        src = piece_of(0, 0, k)
-        for da in shifts1:
-            copy_a(da, src, k).start()
-        for db in shifts2:
-            copy_b(db, src, k).start()
-        copy_p(src).start()
-
+            step(pl.multiple_of(cuts[k][0] + g * 16, 16), 16, pl.ds(0, width), True)
+
+        gather.own(k)
+    step(0, first, pl.ds(0, early), False)
+
+    for k in range(halves):
+        ahead.last(k)
+    everyone.wait_send()
     for k in range(pieces):
-        for da in shifts1:
-            src = piece_of(n1 - da, 0, k)
-            copy_a(da, src, k).wait_recv()
-            for db in shifts2:
-                copy_f(da, db, src, k).start()
-            copy_p(src).start()
-        for db in shifts2:
-            src = piece_of(0, n2 - db, k)
-            copy_b(db, src, k).wait_recv()
-            copy_p(src).start()
+        gather.forward(k)
+        if k == min(1, pieces - 1):
+            half = terms.at[pl.ds(0, blocks)]
+            remote(half, half, q_s, qp_r, partner).wait_recv()
+
+            @pl.loop(0, 2 * blocks)
+            def _(i):
+                w, _, _ = adam(*(terms[i, j].astype(F32) for j in range(4)))
+                w_out[pl.ds(pl.multiple_of(i * rows, rows), first), pl.ds(0, early)] = w.astype(BF16)
+
     for k in range(pieces):
-        for da in shifts1:
-            for db in shifts2:
-                src = piece_of(n1 - da, n2 - db, k)
-                copy_f(da, db, src, k).wait_recv()
-                copy_p(src).start()
-
-    half = w_out.at[pl.ds(0, n1 * n2 * rows)]
-    remote(half, half, p_s, p_r, partner).wait_recv()
-    remote(half, half, p_s, p_r, partner).wait_send()
-    remote(peer, peer, peer_s, peer_r.at[0], partner).wait_send()
-    remote(part1, land1, s1, r1.at[0], partner).wait_send()
-    remote(part2, land2, s2, r2.at[0], partner).wait_send()
-    for sem, count, recv in ((a_s, n1 - 1, a_r), (b_s, n2 - 1, b_r), (f_s, (n1 - 1) * (n2 - 1), f_r)):
-        ref = w_out.at[pl.ds(0, count * rows)]
-        remote(ref, ref, sem, recv.at[0], partner).wait_send()
+        gather.last(k)
+
+    def sized(count, first_piece):
+        if first_piece:
+            return w_out.at[pl.ds(0, count * first), pl.ds(early, width - early)]
+        return w_out.at[pl.ds(0, count * (rows - first))]
+
+    sent = terms.at[pl.ds(0, 2 * blocks - 1)]
+    remote(sent, sent, q_s, qp_r, partner).wait_send()
+    for first_piece, send, land in ((True, h_s, h_r), (False, g_s, g_r)):
+        ref = sized(blocks, first_piece)
+        remote(ref, ref, send, land, partner).wait_recv()
+        ref = sized(2 * blocks - 1, first_piece)
+        remote(ref, ref, send, land, partner).wait_send()
     if staged:
         final = pltpu.make_async_copy(w_out, w_hbm, w_sem)
         final.start()
@@ -303,30 +370,29 @@
     regular = pltpu.SemaphoreType.REGULAR
     block = lambda n, dtype=BF16: pltpu.VMEM((n, rows, width), dtype)
     state = lambda: pltpu.VMEM((rows, width), F32)
+    early = max(128, width // EARLY // 128 * 128)
     scratch = [
         block(blocks), block(blocks),
         block((n1 - 1) * n2), block((n1 - 1) * n2),
         block(n2 - 1), block(n2 - 1),
-        state(), state(), state(), state(),
+        state(), pltpu.VMEM((3, rows, width), F32),
         pltpu.VMEM((devices, 1, 128), F32),
-        dma(blocks * pieces), dma(3), one, dma(blocks * pieces),
-        one, dma((n1 - 1) * n2 * pieces), one, dma((n2 - 1) * pieces),
-        one, one,
-        one, dma((n1 - 1) * pieces), one, dma((n2 - 1) * pieces),
-        one, dma((n1 - 1) * (n2 - 1) * pieces),
-        one, one,
+        pltpu.VMEM((2 * blocks, 4, sizes[0], early), BF16),
+        dma(blocks), dma(3), one, dma((n1 - 1) * (n2 - 1) * (pieces - 1) + blocks),
+        one, one, dma((blocks - 1) * pieces),
+        one, one, one, dma((blocks - 1) * 2), one, one, one, one, one,
         regular, regular, regular, regular, regular,
     ]
     block_bytes = rows * width * 2
     staged = rows_tp * width * 2 > 8 << 20
     if staged:
         scratch += [pltpu.VMEM((rows_tp, width), BF16), one]
-    limit = block_bytes * (2 * blocks + 2 * (n1 - 1) * n2 + 2 * (n2 - 1) + 8 + staged * ends * dps) + devices * 4096 + (3 << 20)
+    limit = block_bytes * (2 * blocks + 2 * (n1 - 1) * n2 + 2 * (n2 - 1) + 8 + staged * ends * dps) + devices * 4096 + 2 * blocks * 8 * sizes[0] * early + (3 << 20)
     stays = pl.BlockSpec(memory_space=pltpu.HBM)
     vmem = pl.BlockSpec(memory_space=pltpu.VMEM)
     vmem_any = pl.BlockSpec(memory_space=pl.ANY)
     results = pl.pallas_call(
-        functools.partial(kernel, (ends, ys, tps, rows, width, cuts, staged)),
+        functools.partial(kernel, (ends, ys, tps, rows, width, cuts, early, staged)),
         out_shape=(
             (pltpu.HBM if staged else pltpu.VMEM)((rows_tp, width), BF16),
             pltpu.VMEM((rows, width), F32),

time: 71.8 us -> 70.6 us (0.983)
  Pallas kernels: 71 us -> 69.8 us
    pallas_call x1, Pallas kernels: 66.8 us -> 65.6 us  [per_device(): pl.pallas_call(functools.partial(kernel, (ends, ys, tps, rows, width, cut...]
where the time goes in v2:
time: 70.6 us; the launch traced here: 70.5 us
  Pallas kernels  69.8 us (99%)
    pallas_call x1, Pallas kernels, per_device(): pl.pallas_call(functools.partial(kernel, (ends, ys, tps, rows, width, cut...  65.6 us
    pallas_call x1, Pallas kernels, per_device(): pl.pallas_call(put_out, out_shape=tuple((pltpu.HBM(x.shape, x.dtype) for...  4.2 us

profile of v2, /device:TPU:0, one launch (start us, length us, event | category | flops | bytes accessed | tf_op | source)
XLA Modules:
  0.0 70.5 jit_solution(5379402019411162000)
XLA Ops:
  0.6 65.6 %sum_update_gather.1 = (bf16[1024,3072]{1,0:T(8,128)(2,1)S(1)}, f32[128,3072]{1,0:T(8,128)S(1)}, f32[128,3072]{1,0:T(8,128)S(1)}, f32[128,3072]{1,0:T(8,128)S(1)}) custom-call(bf16[1024,3072]{1,0:T(8,128)(2,1)} %bitcast.7, f32[128,3072]{1,0:T(8,128)} %bitcast.8, f32[128,3072]{1,0:T(8,128)} %bitcast.9, f32[128,3072]{1,0:T(8,128)} %bitcast.10), custom_call_target="tpu_custom_call" | custom-call | tf_op jit(solution)/shard_map/sum_update_gather/pallas_call | solution.py:394
  66.3 4.2 %put_out.1 = (bf16[1024,3072]{1,0:T(8,128)(2,1)}, f32[128,3072]{1,0:T(8,128)}, f32[128,3072]{1,0:T(8,128)}, f32[128,3072]{1,0:T(8,128)}) custom-call(bf16[1024,3072]{1,0:T(8,128)(2,1)S(1)} %get-tuple-element.12.refs_0_, f32[128,3072]{1,0:T(8,128)S(1)} %get-tuple-element.13.refs_1_, f32[128,3072]{1,0:T(8,128)S(1)} %get-tuple-element.14.refs_2_, ...), custom_call_target="tpu_custom_call" | custom-call | tf_op jit(solution)/shard_map/put_out/pallas_call | solution.py:410

commit v3 on v2

--- a/solution.py
+++ b/solution.py
@@ -12,7 +12,7 @@
 MESH = pl.DeviceIdType.MESH
 F32 = jnp.float32
 BF16 = jnp.bfloat16
-EARLY = 4
+EARLY = 3
 
 
 def remote(src, dst, send, recv, device):
@@ -22,10 +22,10 @@
 
 
 def kernel(cfg, grad, master, moment, second, w_out, master_out, moment_out, second_out, *scratch):
-    ends, ys, tps, rows, width, cuts, early, staged = cfg
+    ends, ys, tps, rows, width, cuts, early, raw, staged = cfg
     if staged:
         w_hbm, (w_out, w_sem), scratch = w_out, scratch[-2:], scratch[:-2]
-    (own, peer, part1, land1, part2, land2, total, states, squares, terms,
+    (lead, extra, lead_sem, raw_r, own, peer, part1, land1, part2, land2, total, states, squares, terms,
      own_sem, st_sem, peer_s, peer_r, s1, s2, recv, ns, nr, q_s, q_r, qp_r, g_s, g_r, h_s, h_r,
      up, down, here_p, here_1, here_2) = scratch
     e, dp, t = lax.axis_index("ends"), lax.axis_index("dp"), lax.axis_index("tp")
@@ -70,7 +70,11 @@
     above, below = {"tp": t + 1}, {"tp": t - 1}
     has_above, has_below = t < tps - 1, t > 0
 
-    for device in planes[0] + planes[1] + [partner]:
+    def across(core, da):
+        ee, yy = place(core, da, 0)
+        return {"ends": ee, "dp": yy * 2 + (1 - c)}
+
+    for device in planes[0] + [across(c, da) for da in shifts1] + planes[1] + [partner]:
         signal(barrier, device)
     pl.when(has_above)(lambda: signal(barrier, above))
     pl.when(has_below)(lambda: signal(barrier, below))
@@ -83,26 +87,50 @@
         i = slot(da, db)
         return pltpu.make_async_copy(grad.at[pl.ds(first_row(c, da, db), rows)], own.at[i], own_sem.at[i])
 
-    for da, db in order:
+    first_raw = (pl.ds(0, first), pl.ds(0, raw))
+    leads = [
+        pltpu.make_async_copy(grad.at[rows_at(first_row(1 - c, da, db), 0), pl.ds(0, raw)], lead.at[i], lead_sem.at[i])
+        for i, (da, db) in enumerate(corners)
+    ]
+    for copy in leads:
+        copy.start()
+    for da, db in corners:
         own_copy(da, db).start()
     state_copies = [
         pltpu.make_async_copy(src, states.at[i], st_sem.at[i]) for i, src in enumerate((master, moment, second))
     ]
-    pl.semaphore_wait(barrier, n1 + n2 - 1 + has_above.astype(jnp.int32) + has_below.astype(jnp.int32))
+    for copy in leads + [own_copy(da, db) for da, db in corners]:
+        copy.wait()
+    pl.semaphore_wait(barrier, 2 * n1 + n2 - 2 + has_above.astype(jnp.int32) + has_below.astype(jnp.int32))
 
     def peer_copy(da, db, k):
         i, start = slot(da, db), first_row(1 - c, da, db)
         if da and db:
             sem = peer_r.at[corners.index((da, db)) * pieces + k]
-            return remote(grad.at[rows_at(start, k)], peer.at[i, part(k)], peer_s, sem, partner)
+            columns = sum_columns(da, db, k)
+            return remote(grad.at[rows_at(start, k), columns], peer.at[i, part(k), columns], peer_s, sem, partner)
         sem = peer_r.at[len(corners) * pieces + order.index((da, db)) - len(corners)]
         return remote(grad.at[pl.ds(start, rows)], peer.at[i], peer_s, sem, partner)
 
     cut = lambda da, db: pieces if da and db else 1
+
+    def sum_columns(da, db, k):
+        return pl.ds(raw, width - raw) if da and db and k == 0 else pl.ds(0, width)
+
+    def raw_copies(i, da, db):
+        j = (da - 1) * n2 + db
+        mine = remote(own.at[slot(da, db), *first_raw], land1.at[j, *first_raw], s1, raw_r.at[2 * i], at(da, 0))
+        return mine, remote(lead.at[i], extra.at[i], peer_s, raw_r.at[2 * i + 1], across(1 - c, da))
+
+    for i, (da, db) in enumerate(corners):
+        for copy in raw_copies(i, da, db):
+            copy.start()
 
     for da, db in order:
         for k in range(cut(da, db)):
             peer_copy(da, db, k).start()
+    for da, db in order[len(corners):]:
+        own_copy(da, db).start()
     for copy in state_copies:
         copy.start()
     pl.when(jnp.logical_and(has_above, t == 0))(lambda: signal(up, above))
@@ -133,28 +161,36 @@
 
     def chip_sum(da, db, k):
         i = slot(da, db)
-        if k == 0:
+        if k == 0 and not (da and db):
             own_copy(da, db).wait()
         if k < cut(da, db):
             peer_copy(da, db, k).wait_recv()
-        return own[i, part(k), :].astype(F32) + peer[i, part(k), :].astype(F32)
+        columns = sum_columns(da, db, k)
+        return own[i, part(k), columns].astype(F32) + peer[i, part(k), columns].astype(F32)
 
     def copy1(da, db, k):
         i = (da - 1) * n2 + db
-        return remote(part1.at[i, part(k)], land1.at[i, part(k)], s1, recv.at[i * pieces + k], at(da, 0))
+        columns = sum_columns(da, db, k)
+        return remote(part1.at[i, part(k), columns], land1.at[i, part(k), columns], s1, recv.at[i * pieces + k], at(da, 0))
 
     def copy2(db, k):
         i = db - 1
         return remote(part2.at[i, part(k)], land2.at[i, part(k)], s2, recv.at[((n1 - 1) * n2 + i) * pieces + k], at(0, db))
 
     def send1(da, db, k):
-        part1[(da - 1) * n2 + db, part(k), :] = chip_sum(da, db, k).astype(BF16)
+        part1[(da - 1) * n2 + db, part(k), sum_columns(da, db, k)] = chip_sum(da, db, k).astype(BF16)
         copy1(da, db, k).start()
 
     def sum1(db, k):
         value = chip_sum(0, db, k)
         for da in shifts1:
             copy1(da, db, k).wait_recv()
+            if db and k == 0:
+                i = corners.index((da, db))
+                for copy in raw_copies(i, da, db):
+                    copy.wait_recv()
+                there = extra[i].astype(F32)
+                value = jnp.concatenate([value[:, :raw] + there, value[:, raw:]], axis=1)
             value = value + land1[(da - 1) * n2 + db, part(k), :].astype(F32)
         return value
 
@@ -177,6 +213,60 @@
     mine = member(c, 0, 0)
     for i in range(3):
         terms[mine, i] = states[i, pl.ds(0, first), pl.ds(0, early)].astype(BF16)
+    class Gather:
+        def __init__(self, src, count, send, sems, send_p, recv_p):
+            self.src, self.count, self.sems, self.send, self.send_p, self.recv_p = src, count, sems, send, send_p, recv_p
+
+        def copy(self, i, da, db, k, device):
+            ref = self.src(da, db, k)
+            return remote(ref, ref, self.send(k), self.sems.at[i * self.count + k], device)
+
+        def a(self, da, from_da, k):
+            return self.copy(da - 1, from_da, 0, k, at(da, 0))
+
+        def b(self, db, from_db, k):
+            return self.copy(n1 - 2 + db, 0, from_db, k, at(0, db))
+
+        def f(self, da, db, from_da, from_db, k):
+            return self.copy(n1 + n2 - 2 + (da - 1) * (n2 - 1) + db - 1, from_da, from_db, k, at(0, db))
+
+        def p(self, da, db, k):
+            ref = self.src(da, db, k)
+            remote(ref, ref, self.send_p(k), self.recv_p(k), partner).start()
+
+        def own(self, k):
+            for da in shifts1:
+                self.a(da, 0, k).start()
+            for db in shifts2:
+                self.b(db, 0, k).start()
+            self.p(0, 0, k)
+
+        def forward(self, k):
+            for da in shifts1:
+                self.a(da, n1 - da, k).wait_recv()
+                for db in shifts2:
+                    self.f(da, db, n1 - da, 0, k).start()
+                self.p(n1 - da, 0, k)
+            for db in shifts2:
+                self.b(db, n2 - db, k).wait_recv()
+                self.p(0, n2 - db, k)
+
+        def last(self, k):
+            for da in shifts1:
+                for db in shifts2:
+                    self.f(da, db, n1 - da, n2 - db, k).wait_recv()
+                    self.p(n1 - da, n2 - db, k)
+
+    halves = 2
+    quarter = lambda da, db, k: terms.at[member(c, da, db), pl.ds(4 // halves * k, 4 // halves)]
+    ahead = Gather(quarter, halves, lambda k: q_s, q_r, lambda k: q_s, lambda k: qp_r)
+
+    def piece_of(da, db, k):
+        here = rows_at(first_row(c, da, db), k)
+        return w_out.at[here, pl.ds(early, width - early)] if k == 0 else w_out.at[here]
+
+    gather = Gather(piece_of, pieces, lambda k: g_s if k else h_s, recv, lambda k: g_s if k else h_s, lambda k: g_r if k else h_r)
+
     meet(4)
     acc = jnp.zeros((8, width), F32)
     for k in range(pieces):
@@ -190,6 +280,8 @@
         value = value * value
         for r in range(0, cuts[k][1], 8):
             acc = acc + value[r : r + 8, :]
+        if k == pieces - 2:
+            ahead.own(0)
 
     lanes = acc[:, :128]
     for j in range(128, width, 128):
@@ -209,62 +301,7 @@
                 device = {"ends": lax.rem(e + de, ends), "dp": lax.rem(dp + ddp, ys * 2)}
                 remote(squares.at[me], squares.at[me], ns, nr, device).start()
 
-    class Gather:
-        def __init__(self, src, count, send, sems, send_p, recv_p):
-            self.src, self.count, self.sems, self.send, self.send_p, self.recv_p = src, count, sems, send, send_p, recv_p
-
-        def copy(self, i, da, db, k, device):
-            ref = self.src(da, db, k)
-            return remote(ref, ref, self.send(k), self.sems.at[i * self.count + k], device)
-
-        def a(self, da, from_da, k):
-            return self.copy(da - 1, from_da, 0, k, at(da, 0))
-
-        def b(self, db, from_db, k):
-            return self.copy(n1 - 2 + db, 0, from_db, k, at(0, db))
-
-        def f(self, da, db, from_da, from_db, k):
-            return self.copy(n1 + n2 - 2 + (da - 1) * (n2 - 1) + db - 1, from_da, from_db, k, at(0, db))
-
-        def p(self, da, db, k):
-            ref = self.src(da, db, k)
-            remote(ref, ref, self.send_p(k), self.recv_p(k), partner).start()
-
-        def own(self, k):
-            for da in shifts1:
-                self.a(da, 0, k).start()
-            for db in shifts2:
-                self.b(db, 0, k).start()
-            self.p(0, 0, k)
-
-        def forward(self, k):
-            for da in shifts1:
-                self.a(da, n1 - da, k).wait_recv()
-                for db in shifts2:
-                    self.f(da, db, n1 - da, 0, k).start()
-                self.p(n1 - da, 0, k)
-            for db in shifts2:
-                self.b(db, n2 - db, k).wait_recv()
-                self.p(0, n2 - db, k)
-
-        def last(self, k):
-            for da in shifts1:
-                for db in shifts2:
-                    self.f(da, db, n1 - da, n2 - db, k).wait_recv()
-                    self.p(n1 - da, n2 - db, k)
-
-    halves = 2
-    quarter = lambda da, db, k: terms.at[member(c, da, db), pl.ds(4 // halves * k, 4 // halves)]
-    ahead = Gather(quarter, halves, lambda k: q_s, q_r, lambda k: q_s, lambda k: qp_r)
-
-    def piece_of(da, db, k):
-        here = rows_at(first_row(c, da, db), k)
-        return w_out.at[here, pl.ds(early, width - early)] if k == 0 else w_out.at[here]
-
-    gather = Gather(piece_of, pieces, lambda k: g_s if k else h_s, recv, lambda k: g_s if k else h_s, lambda k: g_r if k else h_r)
-
-    for k in range(halves):
-        ahead.own(k)
+    ahead.own(1)
     for k in range(halves):
         ahead.forward(k)
     remote(peer, peer, peer_s, peer_r.at[0], partner).wait_send()
@@ -371,7 +408,11 @@
     block = lambda n, dtype=BF16: pltpu.VMEM((n, rows, width), dtype)
     state = lambda: pltpu.VMEM((rows, width), F32)
     early = max(128, width // EARLY // 128 * 128)
+    raw = max(128, width * 2 // 3 // 128 * 128)
+    corners = (n1 - 1) * (n2 - 1)
+    ahead = lambda: pltpu.VMEM((corners, sizes[0], raw), BF16)
     scratch = [
+        ahead(), ahead(), dma(corners), dma(2 * corners),
         block(blocks), block(blocks),
         block((n1 - 1) * n2), block((n1 - 1) * n2),
         block(n2 - 1), block(n2 - 1),
@@ -387,12 +428,12 @@
     staged = rows_tp * width * 2 > 8 << 20
     if staged:
         scratch += [pltpu.VMEM((rows_tp, width), BF16), one]
-    limit = block_bytes * (2 * blocks + 2 * (n1 - 1) * n2 + 2 * (n2 - 1) + 8 + staged * ends * dps) + devices * 4096 + 2 * blocks * 8 * sizes[0] * early + (3 << 20)
+    limit = block_bytes * (2 * blocks + 2 * (n1 - 1) * n2 + 2 * (n2 - 1) + 8 + staged * ends * dps) + devices * 4096 + 2 * blocks * 8 * sizes[0] * early + 4 * corners * sizes[0] * raw + (3 << 20)
     stays = pl.BlockSpec(memory_space=pltpu.HBM)
     vmem = pl.BlockSpec(memory_space=pltpu.VMEM)
     vmem_any = pl.BlockSpec(memory_space=pl.ANY)
     results = pl.pallas_call(
-        functools.partial(kernel, (ends, ys, tps, rows, width, cuts, early, staged)),
+        functools.partial(kernel, (ends, ys, tps, rows, width, cuts, early, raw, staged)),
         out_shape=(
             (pltpu.HBM if staged else pltpu.VMEM)((rows_tp, width), BF16),
             pltpu.VMEM((rows, width), F32),

time: 70.6 us -> 70.2 us (level)
  no operation moved by 1% of the time
where the time goes in v3:
time: 70.2 us; the launch traced here: 70 us
  Pallas kernels  69.4 us (99%)
    pallas_call x1, Pallas kernels, per_device(): pl.pallas_call(functools.partial(kernel, (ends, ys, tps, rows, width, cut...  65.2 us
    pallas_call x1, Pallas kernels, per_device(): pl.pallas_call(put_out, out_shape=tuple((pltpu.HBM(x.shape, x.dtype) for...  4.2 us

profile of v3, /device:TPU:0, one launch (start us, length us, event | category | flops | bytes accessed | tf_op | source)
XLA Modules:
  0.0 70.0 jit_solution(11061309370642258658)
XLA Ops:
  0.6 65.2 %sum_update_gather.1 = (bf16[1024,3072]{1,0:T(8,128)(2,1)S(1)}, f32[128,3072]{1,0:T(8,128)S(1)}, f32[128,3072]{1,0:T(8,128)S(1)}, f32[128,3072]{1,0:T(8,128)S(1)}) custom-call(bf16[1024,3072]{1,0:T(8,128)(2,1)} %bitcast.7, f32[128,3072]{1,0:T(8,128)} %bitcast.8, f32[128,3072]{1,0:T(8,128)} %bitcast.9, f32[128,3072]{1,0:T(8,128)} %bitcast.10), custom_call_target="tpu_custom_call" | custom-call | tf_op jit(solution)/shard_map/sum_update_gather/pallas_call | solution.py:435
  65.8 4.2 %put_out.1 = (bf16[1024,3072]{1,0:T(8,128)(2,1)}, f32[128,3072]{1,0:T(8,128)}, f32[128,3072]{1,0:T(8,128)}, f32[128,3072]{1,0:T(8,128)}) custom-call(bf16[1024,3072]{1,0:T(8,128)(2,1)S(1)} %get-tuple-element.12.refs_0_, f32[128,3072]{1,0:T(8,128)S(1)} %get-tuple-element.13.refs_1_, f32[128,3072]{1,0:T(8,128)S(1)} %get-tuple-element.14.refs_2_, ...), custom_call_target="tpu_custom_call" | custom-call | tf_op jit(solution)/shard_map/put_out/pallas_call | solution.py:451

commit v4 on v3

--- a/solution.py
+++ b/solution.py
@@ -12,7 +12,7 @@
 MESH = pl.DeviceIdType.MESH
 F32 = jnp.float32
 BF16 = jnp.bfloat16
-EARLY = 3
+EARLY = 2
 
 
 def remote(src, dst, send, recv, device):
@@ -25,9 +25,8 @@
     ends, ys, tps, rows, width, cuts, early, raw, staged = cfg
     if staged:
         w_hbm, (w_out, w_sem), scratch = w_out, scratch[-2:], scratch[:-2]
-    (lead, extra, lead_sem, raw_r, own, peer, part1, land1, part2, land2, total, states, squares, terms,
-     own_sem, st_sem, peer_s, peer_r, s1, s2, recv, ns, nr, q_s, q_r, qp_r, g_s, g_r, h_s, h_r,
-     up, down, here_p, here_1, here_2) = scratch
+    (lead, extra, lead_sem, own, peer, part1, land1, part2, land2, total, states, squares, terms,
+     own_sem, st_sem, peer_s, peer_r, s1, s2, recv, ns, nr, q_s, up, down, here_p, here_1, here_2) = scratch
     e, dp, t = lax.axis_index("ends"), lax.axis_index("dp"), lax.axis_index("tp")
     y, c = dp // 2, lax.rem(dp, 2)
     pieces = len(cuts)
@@ -89,18 +88,19 @@
 
     first_raw = (pl.ds(0, first), pl.ds(0, raw))
     leads = [
-        pltpu.make_async_copy(grad.at[rows_at(first_row(1 - c, da, db), 0), pl.ds(0, raw)], lead.at[i], lead_sem.at[i])
+        pltpu.make_async_copy(grad.at[rows_at(first_row(core, da, db), 0), pl.ds(0, raw)], lead.at[2 * i + j], lead_sem.at[2 * i + j])
         for i, (da, db) in enumerate(corners)
+        for j, core in enumerate((c, 1 - c))
     ]
     for copy in leads:
         copy.start()
+    state_copies = [
+        pltpu.make_async_copy(src, states.at[i], st_sem) for i, src in enumerate((master, moment, second))
+    ]
+    for copy in leads:
+        copy.wait()
     for da, db in corners:
         own_copy(da, db).start()
-    state_copies = [
-        pltpu.make_async_copy(src, states.at[i], st_sem.at[i]) for i, src in enumerate((master, moment, second))
-    ]
-    for copy in leads + [own_copy(da, db) for da, db in corners]:
-        copy.wait()
     pl.semaphore_wait(barrier, 2 * n1 + n2 - 2 + has_above.astype(jnp.int32) + has_below.astype(jnp.int32))
 
     def peer_copy(da, db, k):
@@ -109,7 +109,8 @@
             sem = peer_r.at[corners.index((da, db)) * pieces + k]
             columns = sum_columns(da, db, k)
             return remote(grad.at[rows_at(start, k), columns], peer.at[i, part(k), columns], peer_s, sem, partner)
-        sem = peer_r.at[len(corners) * pieces + order.index((da, db)) - len(corners)]
+        last = peer_r.shape[0] - 1
+        sem = peer_r.at[len(corners) * pieces + order.index((da, db)) - len(corners) if da or db else last]
         return remote(grad.at[pl.ds(start, rows)], peer.at[i], peer_s, sem, partner)
 
     cut = lambda da, db: pieces if da and db else 1
@@ -119,8 +120,8 @@
 
     def raw_copies(i, da, db):
         j = (da - 1) * n2 + db
-        mine = remote(own.at[slot(da, db), *first_raw], land1.at[j, *first_raw], s1, raw_r.at[2 * i], at(da, 0))
-        return mine, remote(lead.at[i], extra.at[i], peer_s, raw_r.at[2 * i + 1], across(1 - c, da))
+        mine = remote(lead.at[2 * i], land1.at[j, *first_raw], s1, recv.at[(blocks - 1) * pieces + 2 * i], at(da, 0))
+        return mine, remote(lead.at[2 * i + 1], extra.at[i], peer_s, recv.at[(blocks - 1) * pieces + 2 * i + 1], across(1 - c, da))
 
     for i, (da, db) in enumerate(corners):
         for copy in raw_copies(i, da, db):
@@ -161,7 +162,7 @@
 
     def chip_sum(da, db, k):
         i = slot(da, db)
-        if k == 0 and not (da and db):
+        if k == 0:
             own_copy(da, db).wait()
         if k < cut(da, db):
             peer_copy(da, db, k).wait_recv()
@@ -208,14 +209,13 @@
             meet(k)
     for step in range(min(pieces, 3), 4):
         meet(step)
-    for copy in state_copies:
-        copy.wait()
+    remote(states, states, st_sem, st_sem, partner).wait_recv()
     mine = member(c, 0, 0)
     for i in range(3):
         terms[mine, i] = states[i, pl.ds(0, first), pl.ds(0, early)].astype(BF16)
     class Gather:
-        def __init__(self, src, count, send, sems, send_p, recv_p):
-            self.src, self.count, self.sems, self.send, self.send_p, self.recv_p = src, count, sems, send, send_p, recv_p
+        def __init__(self, src, count, send, sems, recv_p, to_both=None):
+            self.src, self.count, self.sems, self.send, self.recv_p, self.to_both = src, count, sems, send, recv_p, to_both
 
         def copy(self, i, da, db, k, device):
             ref = self.src(da, db, k)
@@ -232,7 +232,7 @@
 
         def p(self, da, db, k):
             ref = self.src(da, db, k)
-            remote(ref, ref, self.send_p(k), self.recv_p(k), partner).start()
+            remote(ref, ref, self.send(k), self.recv_p(k), partner).start()
 
         def own(self, k):
             for da in shifts1:
@@ -241,11 +241,18 @@
                 self.b(db, 0, k).start()
             self.p(0, 0, k)
 
+        def twin(self, db):
+            ee, yy = place(c, 0, db)
+            return {"ends": ee, "dp": yy * 2 + (1 - c)}
+
         def forward(self, k):
             for da in shifts1:
                 self.a(da, n1 - da, k).wait_recv()
                 for db in shifts2:
                     self.f(da, db, n1 - da, 0, k).start()
+                    if k == self.to_both:
+                        ref = self.src(n1 - da, 0, k)
+                        remote(ref, ref, self.send(k), self.recv_p(k), self.twin(db)).start()
                 self.p(n1 - da, 0, k)
             for db in shifts2:
                 self.b(db, n2 - db, k).wait_recv()
@@ -255,17 +262,27 @@
             for da in shifts1:
                 for db in shifts2:
                     self.f(da, db, n1 - da, n2 - db, k).wait_recv()
-                    self.p(n1 - da, n2 - db, k)
-
-    halves = 2
+                    if k != self.to_both:
+                        self.p(n1 - da, n2 - db, k)
+
+    halves = 4
     quarter = lambda da, db, k: terms.at[member(c, da, db), pl.ds(4 // halves * k, 4 // halves)]
-    ahead = Gather(quarter, halves, lambda k: q_s, q_r, lambda k: q_s, lambda k: qp_r)
+    qp_r = own_sem.at[blocks - 1]
+    ahead = Gather(quarter, halves, lambda k: q_s, peer_r, lambda k: qp_r)
+
+    tail = width // 256 * 128
 
     def piece_of(da, db, k):
-        here = rows_at(first_row(c, da, db), k)
-        return w_out.at[here, pl.ds(early, width - early)] if k == 0 else w_out.at[here]
-
-    gather = Gather(piece_of, pieces, lambda k: g_s if k else h_s, recv, lambda k: g_s if k else h_s, lambda k: g_r if k else h_r)
+        start = first_row(c, da, db)
+        if k == 0:
+            return w_out.at[rows_at(start, 0), pl.ds(early, width - early)]
+        if k < pieces - 1:
+            return w_out.at[rows_at(start, k)]
+        return w_out.at[rows_at(start, pieces - 1), pl.ds(0, tail) if k == pieces - 1 else pl.ds(tail, width - tail)]
+
+    group = lambda k: 0 if k == 0 else 1 if k < pieces - 1 else 2
+    sends, lands = (s2, s1, peer_s), [own_sem.at[i] for i in range(3)]
+    gather = Gather(piece_of, pieces + 1, lambda k: sends[group(k)], recv, lambda k: lands[group(k)], pieces)
 
     meet(4)
     acc = jnp.zeros((8, width), F32)
@@ -281,7 +298,10 @@
         for r in range(0, cuts[k][1], 8):
             acc = acc + value[r : r + 8, :]
         if k == pieces - 2:
-            ahead.own(0)
+            @pl.when(t < tps // 2)
+            def _():
+                for i in range(3):
+                    ahead.own(i)
 
     lanes = acc[:, :128]
     for j in range(128, width, 128):
@@ -301,7 +321,13 @@
                 device = {"ends": lax.rem(e + de, ends), "dp": lax.rem(dp + ddp, ys * 2)}
                 remote(squares.at[me], squares.at[me], ns, nr, device).start()
 
-    ahead.own(1)
+    @pl.when(t >= tps // 2)
+    def _():
+        for i in range(3):
+            ahead.own(i)
+
+    for i in range(3, halves):
+        ahead.own(i)
     for k in range(halves):
         ahead.forward(k)
     remote(peer, peer, peer_s, peer_r.at[0], partner).wait_send()
@@ -341,14 +367,15 @@
             step(pl.multiple_of(cuts[k][0] + g * 16, 16), 16, pl.ds(0, width), True)
 
         gather.own(k)
+    gather.own(pieces)
     step(0, first, pl.ds(0, early), False)
 
     for k in range(halves):
         ahead.last(k)
     everyone.wait_send()
-    for k in range(pieces):
+    for k in range(pieces + 1):
         gather.forward(k)
-        if k == min(1, pieces - 1):
+        if k == 1:
             half = terms.at[pl.ds(0, blocks)]
             remote(half, half, q_s, qp_r, partner).wait_recv()
 
@@ -357,21 +384,21 @@
                 w, _, _ = adam(*(terms[i, j].astype(F32) for j in range(4)))
                 w_out[pl.ds(pl.multiple_of(i * rows, rows), first), pl.ds(0, early)] = w.astype(BF16)
 
-    for k in range(pieces):
+    for k in range(pieces + 1):
         gather.last(k)
 
-    def sized(count, first_piece):
-        if first_piece:
+    def sized(count, k):
+        if k == 0:
             return w_out.at[pl.ds(0, count * first), pl.ds(early, width - early)]
-        return w_out.at[pl.ds(0, count * (rows - first))]
+        return w_out.at[pl.ds(0, count * (rows - first - cuts[-1][1] if k == 1 else cuts[-1][1]))]
 
     sent = terms.at[pl.ds(0, 2 * blocks - 1)]
     remote(sent, sent, q_s, qp_r, partner).wait_send()
-    for first_piece, send, land in ((True, h_s, h_r), (False, g_s, g_r)):
-        ref = sized(blocks, first_piece)
-        remote(ref, ref, send, land, partner).wait_recv()
-        ref = sized(2 * blocks - 1, first_piece)
-        remote(ref, ref, send, land, partner).wait_send()
+    for k in (1, 0, 2):
+        ref = sized(blocks, k)
+        remote(ref, ref, sends[k], lands[k], partner).wait_recv()
+        ref = sized(2 * blocks - 1, k)
+        remote(ref, ref, sends[k], lands[k], partner).wait_send()
     if staged:
         final = pltpu.make_async_copy(w_out, w_hbm, w_sem)
         final.start()
@@ -410,25 +437,25 @@
     early = max(128, width // EARLY // 128 * 128)
     raw = max(128, width * 2 // 3 // 128 * 128)
     corners = (n1 - 1) * (n2 - 1)
-    ahead = lambda: pltpu.VMEM((corners, sizes[0], raw), BF16)
+    ahead = lambda count: pltpu.VMEM((count, sizes[0], raw), BF16)
     scratch = [
-        ahead(), ahead(), dma(corners), dma(2 * corners),
+        ahead(2 * corners), ahead(corners), dma(2 * corners),
         block(blocks), block(blocks),
         block((n1 - 1) * n2), block((n1 - 1) * n2),
         block(n2 - 1), block(n2 - 1),
         state(), pltpu.VMEM((3, rows, width), F32),
         pltpu.VMEM((devices, 1, 128), F32),
         pltpu.VMEM((2 * blocks, 4, sizes[0], early), BF16),
-        dma(blocks), dma(3), one, dma((n1 - 1) * (n2 - 1) * (pieces - 1) + blocks),
-        one, one, dma((blocks - 1) * pieces),
-        one, one, one, dma((blocks - 1) * 2), one, one, one, one, one,
+        dma(blocks), one, one, dma(max(corners * (pieces - 1) + blocks, (blocks - 1) * 4 + 1)),
+        one, one, dma((blocks - 1) * (pieces + 1)),
+        one, one, one,
         regular, regular, regular, regular, regular,
     ]
     block_bytes = rows * width * 2
     staged = rows_tp * width * 2 > 8 << 20
     if staged:
         scratch += [pltpu.VMEM((rows_tp, width), BF16), one]
-    limit = block_bytes * (2 * blocks + 2 * (n1 - 1) * n2 + 2 * (n2 - 1) + 8 + staged * ends * dps) + devices * 4096 + 2 * blocks * 8 * sizes[0] * early + 4 * corners * sizes[0] * raw + (3 << 20)
+    limit = block_bytes * (2 * blocks + 2 * (n1 - 1) * n2 + 2 * (n2 - 1) + 8 + staged * ends * dps) + devices * 4096 + 2 * blocks * 8 * sizes[0] * early + 6 * corners * sizes[0] * raw + (3 << 20)
     stays = pl.BlockSpec(memory_space=pltpu.HBM)
     vmem = pl.BlockSpec(memory_space=pltpu.VMEM)
     vmem_any = pl.BlockSpec(memory_space=pl.ANY)

time: 70.2 us -> 69.7 us (level)
  no operation moved by 1% of the time
where the time goes in v4:
time: 69.7 us; the launch traced here: 69.5 us
  Pallas kernels  68.9 us (99%)
    pallas_call x1, Pallas kernels, per_device(): pl.pallas_call(functools.partial(kernel, (ends, ys, tps, rows, width, cut...  64.7 us
    pallas_call x1, Pallas kernels, per_device(): pl.pallas_call(put_out, out_shape=tuple((pltpu.HBM(x.shape, x.dtype) for...  4.2 us

profile of v4, /device:TPU:0, one launch (start us, length us, event | category | flops | bytes accessed | tf_op | source)
XLA Modules:
  0.0 69.5 jit_solution(17541999877290011392)
XLA Ops:
  0.6 64.7 %sum_update_gather.1 = (bf16[1024,3072]{1,0:T(8,128)(2,1)S(1)}, f32[128,3072]{1,0:T(8,128)S(1)}, f32[128,3072]{1,0:T(8,128)S(1)}, f32[128,3072]{1,0:T(8,128)S(1)}) custom-call(bf16[1024,3072]{1,0:T(8,128)(2,1)} %bitcast.7, f32[128,3072]{1,0:T(8,128)} %bitcast.8, f32[128,3072]{1,0:T(8,128)} %bitcast.9, f32[128,3072]{1,0:T(8,128)} %bitcast.10), custom_call_target="tpu_custom_call" | custom-call | tf_op jit(solution)/shard_map/sum_update_gather/pallas_call | solution.py:462
  65.3 4.2 %put_out.1 = (bf16[1024,3072]{1,0:T(8,128)(2,1)}, f32[128,3072]{1,0:T(8,128)}, f32[128,3072]{1,0:T(8,128)}, f32[128,3072]{1,0:T(8,128)}) custom-call(bf16[1024,3072]{1,0:T(8,128)(2,1)S(1)} %get-tuple-element.12.refs_0_, f32[128,3072]{1,0:T(8,128)S(1)} %get-tuple-element.13.refs_1_, f32[128,3072]{1,0:T(8,128)S(1)} %get-tuple-element.14.refs_2_, ...), custom_call_target="tpu_custom_call" | custom-call | tf_op jit(solution)/shard_map/put_out/pallas_call | solution.py:478
